TPU v7x, 32 devices: a whole 2x2x4 slice. The times are simulated.
32 devices in a mesh: depth: 8 (over z, x), col: 4 (over y, core).
Axes of the slice: x: 2, y: 2, z: 4, core: 2. Of those that a mesh axis runs over, the one named last changes fastest.
Arguments:
- recorded: bfloat16 [4, 16, 2, 512, 512], P(None, 'depth', None, 'col'), may hold values from -6 to 6
- vertical: float32 [4, 512], replicated, may hold values from 0.05 to 0.8
Outputs:
- prediction: float32 [4, 2, 512, 512], P(None, None, 'col', 'depth')
All inputs are finite; a program needn't handle non-finite values.
Results may differ from a plain program's by a relative error of at most 0.01.
Values may be sent and summed in bfloat16 or wider, within the bound.
A program may use at most 64 MiB of HBM per device.

v0:
```python
import jax
import jax.numpy as jnp
from jax import lax
from jax.sharding import PartitionSpec as P


def prefix(x, axis, combine, identity):
    peers, mine = (lax.axis_size(axis), lax.axis_index(axis))
    everything = lax.all_gather(x, axis)
    start = jnp.broadcast_to(jnp.asarray(identity, x.dtype), x.shape)

    def lap(k, before):
        at = peers - 1 - k
        reached = at > mine
        new = combine(before, everything[at])
        return jnp.where(reached, new, before)

    return lax.fori_loop(0, peers, lap, start)


def from_behind(value, axis, steps):
    count = lax.axis_size(axis)
    initial, last = (max(0, -steps), min(count, count - steps))
    return lax.ppermute(value, axis, [(source, source + steps) for source in range(initial, last)])


def complex_product(left_side, right_side, pattern, stack_axis):
    left_real = left_side[:, :, 0]
    left_imag = left_side[:, :, 1]
    right_real = right_side[:, :, 0]
    right_imag = right_side[:, :, 1]
    real_part = jnp.einsum(
        pattern, left_real, right_real, preferred_element_type=jnp.float32
    ) - jnp.einsum(pattern, left_imag, right_imag, preferred_element_type=jnp.float32)
    imag_part = jnp.einsum(
        pattern, left_real, right_imag, preferred_element_type=jnp.float32
    ) + jnp.einsum(pattern, left_imag, right_real, preferred_element_type=jnp.float32)
    return jnp.stack([real_part, imag_part], axis=stack_axis)


def add_pair(earlier, later):
    return earlier + later


def shards(recorded, vertical):
    local_depths = recorded.shape[1]
    row_count = recorded.shape[3]
    depth_cells = lax.axis_size("depth") * local_depths
    depth_step = 1.0 / depth_cells
    first_row = lax.axis_index("col") * row_count
    row_wave = lax.dynamic_slice_in_dim(vertical, first_row, row_count, 1)
    depth_f = (
        lax.axis_index("depth") * local_depths + jnp.arange(local_depths, dtype=jnp.int32)
    ).astype(jnp.float32)
    phase_angle = (row_wave[:, None, :, None] + vertical[:, None, None, :]) * depth_f[
        None, :, None, None
    ]
    cosine = jnp.cos(phase_angle)
    sine_part = jnp.sin(phase_angle)
    real_in = recorded[:, :, 0].astype(jnp.float32)
    imag_in = recorded[:, :, 1].astype(jnp.float32)
    plus32 = (
        jnp.stack(
            [real_in * cosine - imag_in * sine_part, real_in * sine_part + imag_in * cosine], axis=2
        )
        * depth_step
    )
    minus_phase = (
        jnp.stack(
            [real_in * cosine + imag_in * sine_part, imag_in * cosine - real_in * sine_part], axis=2
        )
        * depth_step
    ).astype(jnp.bfloat16)
    inner_sum = lax.cumsum(plus32, axis=1, reverse=True)
    beyond = prefix(inner_sum[:, 0], "depth", add_pair, jnp.zeros_like(inner_sum[:, 0]))
    suffix_all = inner_sum + beyond[:, None]
    following = from_behind(suffix_all[:, 0], "depth", -1)
    tail_sum = jnp.concatenate([suffix_all[:, 1:], following[:, None]], axis=1).astype(jnp.bfloat16)
    columns = tail_sum
    middle = complex_product(
        columns, lax.all_gather(minus_phase, "col", axis=3, tiled=True), "wzrk,wzkc->wzrc", 2
    ).astype(jnp.bfloat16)
    columns = middle
    partial_pred = complex_product(
        columns, lax.all_gather(tail_sum, "col", axis=3, tiled=True), "wzrk,wzkc->wrc", 1
    )
    return lax.psum_scatter(partial_pred, "depth", scatter_dimension=3, tiled=True)


def solution(mesh):
    in_specs = (P(None, "depth", None, "col", None), P())
    out_specs = P(None, None, "col", "depth")
    return jax.shard_map(shards, mesh=mesh, in_specs=in_specs, out_specs=out_specs, check_vma=False)
```

profile of v0, /device:TPU:8, one launch (start us, length us, event | category | flops | bytes accessed | tf_op | source)
XLA Modules:
  0.0 488.6 jit_solution(11230011602802175978)
XLA Ops:
  7.2 0.8 broadcast_add_fusion.1
  8.1 10.4 %fusion.21 = (f32[4,2,1,128,512]{4,3,1,0,2:T(8,128)S(1)}, f32[4,2,1,128,512]{4,3,1,0,2:T(8,128)S(1)}, f32[4,2,1,128,512]{4,3,1,0,2:T(8,128)S(1)}, f32[4,2,1,128,512]{4,3,1,0,2:T(8,128)}) fusion(f32[2]{0:T(128)S(1)} %add_convert_fusion.1, f32[4,128,512]{2,1,0:T(8,128)S(1)} %broadcast_add_fusion.1, bf16[4,2,2,128,512]{4,3,2,1,0:T(8,128)(2,1)} %param.4), kind=kLoop, calls=%fused_computation.37 | loop fusion | flops 5767168 | bytes 11534344 | tf_op jit(solution)/shard_map/sub | solution.py:64
  18.5 0.9 fusion
  19.4 2.0 copy-done.1
  21.3 1.5 slice.47
  22.9 3.5 fusion.3
  26.5 223.1 %all-gather.9.cloned.1.call-done = f32[32,1,2,128,512]{4,3,1,0,2:T(8,128)} async-done(((f32[4,1,2,128,512]{4,3,1,0,2:T(8,128)}), f32[32,1,2,128,512]{4,3,1,0,2:T(8,128)}) %all-gather.9.cloned.1.call-update) | async-done | bytes 16777232 | tf_op jit(solution)/shard_map/all_gather | solution.py:9
  249.5 19.9 %while.16 = (s32[]{:T(128)}, f32[4,2,128,512]{3,2,1,0:T(8,128)S(1)}, s32[]{:T(128)}, f32[8,4,2,128,512]{4,3,1,0,2:T(8,128)}, s32[]{:T(128)}, /*index=5*/s32[]{:T(128)}, s32[]{:T(128)}, s32[]{:T(128)}) while((s32[]{:T(128)}, f32[4,2,128,512]{3,2,1,0:T(8,128)S(1)}, s32[]{:T(128)}, f32[8,4,2,128,512]{4,3,1,0,2:T(8,128)}, s32[]{:T(128)}, ...), condition=%wide.region_2.3_spmd.clone, body=%wide.region_1.2_spmd.clone.sunk | while | flops 1572872 | bytes 6291611 | solution.py:18
  249.5 2.3 add_select_fusion.2
  251.9 2.3 add_select_fusion.2
  254.2 2.3 add_select_fusion.2
  256.6 2.6 add_select_fusion.2
  259.2 2.7 add_select_fusion.2
  261.9 2.9 add_select_fusion.2
  264.8 2.3 add_select_fusion.2
  267.2 2.3 add_select_fusion.2
  269.5 3.0 broadcast_add_fusion
  272.7 3.8 collective-permute-start
  276.6 22.2 %collective-permute-done = bf16[4,2,128,512]{3,2,0,1:T(8,128)(2,1)S(1)} collective-permute-done((bf16[4,2,128,512]{3,2,0,1:T(8,128)(2,1)S(1)}, bf16[4,2,128,512]{3,2,0,1:T(8,128)(2,1)S(1)}, u32[]{:S(2)}, u32[]{:S(2)}) %collective-permute-start) | collective-permute-done | bytes 1048608 | tf_op jit(solution)/shard_map/ppermute | solution.py:24
  298.8 1.0 copy-done.2
  299.7 1.6 pad_maximum_fusion
  301.4 1.4 fusion.50
  302.8 6.7 %all-gather.5.cloned.1.call-done = bf16[4,2,2,512,512]{4,3,1,0,2:T(8,128)(2,1)} async-done(((bf16[4,2,2,128,512]{4,3,1,0,2:T(8,128)(2,1)}), bf16[4,2,2,512,512]{4,3,1,0,2:T(8,128)(2,1)}) %all-gather.5.cloned.1.call-update) | async-done | bytes 8388624 | tf_op jit(solution)/shard_map/all_gather | solution.py:81
  309.4 3.0 fusion.5
  312.5 3.4 fusion.4
  317.4 51.9 %all-gather.7.cloned.1.call-done = bf16[4,2,2,512,512]{4,3,0,2,1:T(8,128)(2,1)} async-done(((bf16[4,2,2,128,512]{4,3,0,2,1:T(8,128)(2,1)}), bf16[4,2,2,512,512]{4,3,0,2,1:T(8,128)(2,1)}) %all-gather.7.cloned.1.call-update) | async-done | bytes 8388624 | tf_op jit(solution)/shard_map/all_gather | solution.py:85
  369.3 3.8 slice_bitcast_fusion
  375.4 0.8 fusion.40
  376.3 1.9 copy.30
  380.1 100.2 %all-reduce.3.cloned.1.call-done = f32[4,2,128,512]{2,0,1,3:T(4,128)} async-done(((f32[4,2,128,512]{2,0,1,3:T(4,128)}), f32[4,2,128,512]{2,0,1,3:T(4,128)}) %all-reduce.3.cloned.1.call-update) | async-done | bytes 2097168
  480.3 1.0 constant_dynamic-slice_fusion.1
  481.3 0.8 copy.31
  (25 shorter events, 6.1 us)
Async XLA Ops:
  6.5 243.0 %all-gather.9.cloned.1.call-start = ((), (), s32[]{:S(2)}) async-start(), calls=%async_computation.2 | async-start | bytes 18874368 | tf_op jit(solution)/shard_map/all_gather | solution.py:9
  19.4 2.0 copy-start.1
  22.8 286.6 %all-gather.5.cloned.1.call-start = ((), (), s32[]{:S(2)}) async-start(), calls=%async_computation | async-start | bytes 10485760 | tf_op jit(solution)/shard_map/all_gather | solution.py:81
  26.4 342.9 %all-gather.7.cloned.1.call-start = ((), (), s32[]{:S(2)}) async-start(), calls=%async_computation.1 | async-start | bytes 10485760 | tf_op jit(solution)/shard_map/all_gather | solution.py:85
  272.7 26.0 %collective-permute-start = (bf16[4,2,128,512]{3,2,0,1:T(8,128)(2,1)S(1)}, bf16[4,2,128,512]{3,2,0,1:T(8,128)(2,1)S(1)}, u32[]{:S(2)}, u32[]{:S(2)}) collective-permute-start(bf16[4,2,128,512]{3,2,0,1:T(8,128)(2,1)S(1)} %get-tuple-element.155), channel_id=1, source_target_pairs={{4,0},{8,4},{12,8},{16,12},{20,16},{24,20},{28,24},{5,1},{9,5},{13... | collective-permute-start | bytes 3145736 | tf_op jit(solution)/shard_map/ppermute | solution.py:24
  298.8 1.0 copy-start.2
  301.3 179.0 %all-reduce.3.cloned.1.call-start = ((), (), s32[]{:S(2)}) async-start(), calls=%async_computation.3 | async-start | bytes 4194304
  309.4 6.5 %copy-start = (bf16[4,2,2,512,512]{4,3,1,0,2:T(8,128)(2,1)S(1)}, bf16[4,2,2,512,512]{4,3,1,0,2:T(8,128)(2,1)}, u32[]{:S(2)}) copy-start(bf16[4,2,2,512,512]{4,3,1,0,2:T(8,128)(2,1)} %all-gather.5.cloned.1.call-done) | copy-start | bytes 25165828
  378.2 0.7 copy-start.3
Sparse Core Ops, SparseCore 0:
  22.9 226.5 all-gather.8
  251.1 58.2 all-gather.4
  311.0 58.2 all-gather.6
  378.4 101.9 all-reduce.2
where the time goes:
time: 491 us; the launch traced here: 489 us
  waiting for transfers between devices  404 us (82%)
  other arithmetic  41.5 us (8%)
  between operations  14 us (3%)
  local copies, waits for them, and re-layouts  13.9 us (3%)
  matrix products  10.9 us (2%)
    all_gather x1, waiting for transfers between devices, prefix(): everything = lax.all_gather(x, axis)  223 us
    unnamed x5, waiting for transfers between devices  100 us
    all_gather x1, waiting for transfers between devices, shards(): lax.all_gather(tail_sum, 'col', axis=3, tiled=True)  51.9 us
    ppermute x1, waiting for transfers between devices, from_behind(): lax.ppermute(value, axis, [(source, source + steps) for source in range(i...  22.2 us
    select_n x8, other arithmetic, lap(): return jnp.where(reached, new, before)  19.7 us
    sub x1, other arithmetic, shards(): real_in * cosine - imag_in * sine_part  10.4 us
  transfers between devices with their start and end apart: 5, of which 5 were waited for; matrix products, arithmetic and copies ran while one was open for 8% of the time, Pallas kernels for 0%

commit v1 on v0

--- a/solution.py
+++ b/solution.py
@@ -1,7 +1,13 @@
+import functools
+
 import jax
 import jax.numpy as jnp
 from jax import lax
+from jax.experimental import pallas as pl
+from jax.experimental.pallas import tpu as pltpu
 from jax.sharding import PartitionSpec as P
+
+MESH = pl.DeviceIdType.MESH
 
 
 def prefix(x, axis, combine, identity):
@@ -87,7 +93,374 @@
     return lax.psum_scatter(partial_pred, "depth", scatter_dimension=3, tiled=True)
 
 
+def kernel(
+    sizes, rec, ct, rt, out, land, ml, tl, ts, prod, suf, sbuf, srecv, ein, eout, xsend, xrecv,
+    pacc, psend, precv, qsend, qrecv, qsum, fsend, frecv,
+    a_send, a_recv, s_send, s_recv, e_send, e_recv, x_send, x_recv, p_send, p_recv,
+    q_send, q_recv, f_send, f_recv,
+):
+    levels, freqs, cols, local, rows, size, width = sizes
+    depth, col = lax.axis_index("depth"), lax.axis_index("col")
+    z, x = depth // 2, depth % 2
+    y, core = col // 2, col % 2
+    rings = cols // 2
+    half = size // 2
+    chunks = size // width
+    f32, bf16 = jnp.float32, jnp.bfloat16
+
+    def device(zz, xx, yy, cc):
+        return (zz * 2 + xx, yy * 2 + cc)
+
+    other_core = device(z, x, y, 1 - core)
+    barrier = pltpu.get_barrier_semaphore()
+    greeted = 0
+    for dx in range(2):
+        for dc in range(cols):
+            if dx or dc:
+                pl.semaphore_signal(
+                    barrier, inc=1,
+                    device_id=(z * 2 + (x + dx) % 2, (col + dc) % cols), device_id_type=MESH,
+                )
+                greeted += 1
+    for dz in range(1, levels):
+        pl.semaphore_signal(
+            barrier, inc=1, device_id=(((z + dz) % levels) * 2 + x, col), device_id_type=MESH
+        )
+        greeted += 1
+    pl.semaphore_wait(barrier, greeted)
+
+    def remote(src, dst, send, recv, to):
+        return pltpu.make_async_remote_copy(
+            src_ref=src, dst_ref=dst, send_sem=send, recv_sem=recv, device_id=to, device_id_type=MESH
+        )
+
+    def spread(j, dx, dy, near=False):
+        xx, yy = (x + dx) % 2, (y + dy) % rings
+        w = yy * 2 + xx
+        src = rec.at[w, :, :, :, pl.ds(j * width, width)]
+        dst = land.at[:, :, pl.ds(pl.multiple_of(col * rows, rows), rows), pl.ds(j * width, width)]
+        if near:
+            return pltpu.make_async_copy(src, dst, a_recv.at[j, col])
+        return remote(src, dst, a_send.at[j, dy * 2 + dx], a_recv.at[j, col], device(z, xx, yy, x))
+
+    routes = [(dx, dy) for dy in reversed(range(rings)) for dx in (1, 0)]
+    for j in range(chunks):
+        for dx, dy in routes:
+            if dx or dy:
+                spread(j, dx, dy).start()
+            else:
+                pl.when(core == x)(lambda: spread(j, dx, dy, near=True).start())
+                pl.when(core != x)(lambda: spread(j, dx, dy).start())
+
+    @pl.when(z == levels - 1)
+    def _():
+        ein[...] = jnp.zeros_like(ein)
+
+    tile = 64
+
+    def phase(j):
+        for source in range(cols):
+            dst = land.at[:, :, pl.ds(source * rows, rows), pl.ds(j * width, width)]
+            pltpu.make_async_copy(dst, dst, a_recv.at[j, source]).wait()
+        lanes = pl.ds(j * width, width)
+
+        @pl.loop(0, size // tile)
+        def _(t):
+            start = pl.multiple_of(t * tile, tile)
+            at = pl.ds(start, tile)
+            low = pl.ds(start + size, tile)
+            sum_re = sum_im = None
+            for l in reversed(range(local)):
+                if sum_re is not None:
+                    suf[l, 0, at, lanes] = sum_re
+                    suf[l, 1, at, lanes] = sum_im
+                re = land[l, 0, at, lanes].astype(f32)
+                im = land[l, 1, at, lanes].astype(f32)
+                row_cos, row_sin = ct[at, 2 * l : 2 * l + 1], ct[at, 2 * l + 1 : 2 * l + 2]
+                col_cos, col_sin = rt[2 * l : 2 * l + 1, lanes], rt[2 * l + 1 : 2 * l + 2, lanes]
+                cosine = row_cos * col_cos - row_sin * col_sin
+                sine = row_sin * col_cos + row_cos * col_sin
+                a, b, c, d = re * cosine, im * sine, re * sine, im * cosine
+                minus_re, minus_im = a + b, d - c
+                shifted = pl.ds(size + j * width, width)
+                ml[l, at, lanes] = minus_re.astype(bf16)
+                ml[l, low, shifted] = minus_re.astype(bf16)
+                ml[l, at, shifted] = (-minus_im).astype(bf16)
+                ml[l, low, lanes] = minus_im.astype(bf16)
+                plus_re, plus_im = a - b, c + d
+                sum_re = plus_re if sum_re is None else sum_re + plus_re
+                sum_im = plus_im if sum_im is None else sum_im + plus_im
+            sbuf[j, 0, at, :] = sum_re.astype(bf16)
+            sbuf[j, 1, at, :] = sum_im.astype(bf16)
+
+        share(j).start()
+
+    def share(j):
+        theirs = pl.ds(pl.multiple_of((1 - core) * half, half), half)
+        return remote(sbuf.at[j, :, theirs, :], srecv.at[j], s_send.at[j], s_recv.at[j], other_core)
+
+    def down(j):
+        to = device((z + levels - 1) % levels, x, y, core)
+        return remote(eout.at[j], ein.at[j], e_send.at[j], e_recv.at[j], to)
+
+    def across(j):
+        return remote(xsend.at[j], xrecv.at[j], x_send.at[j], x_recv.at[j], other_core)
+
+    def put_tail(j, start, deeper):
+        at, low = pl.ds(start, tile), pl.ds(start + size, tile)
+        lanes = pl.ds(j * width, width)
+        for l in range(local):
+            re, im = deeper
+            if l < local - 1:
+                re, im = re + suf[l, 0, at, lanes], im + suf[l, 1, at, lanes]
+            base = 2 * size * l
+            first = pl.ds(base + j * width, width)
+            second = pl.ds(base + size + j * width, width)
+            ts[l, at, lanes] = re.astype(bf16)
+            ts[l, low, lanes] = im.astype(bf16)
+            tl[at, first] = re.astype(bf16)
+            tl[low, second] = re.astype(bf16)
+            tl[at, second] = (-im).astype(bf16)
+            tl[low, first] = im.astype(bf16)
+
+    def chain(j):
+        share(j).wait_recv()
+        pl.when(z < levels - 1)(lambda: down(j).wait_recv())
+
+        @pl.loop(0, half // tile)
+        def _(t):
+            start = pl.multiple_of(t * tile, tile)
+            at = pl.ds(start, tile)
+            mine = pl.ds(pl.multiple_of(core * half + start, tile), tile)
+            for part in range(2):
+                below = ein[j, part, at, :].astype(f32)
+                own = sbuf[j, part, mine, :].astype(f32)
+                their = srecv[j, part, at, :].astype(f32)
+                eout[j, part, at, :] = (below + own + their).astype(bf16)
+                xsend[j, part, at, :] = (below + jnp.where(core == 1, own, 0.0)).astype(bf16)
+
+        pl.when(z > 0)(lambda: down(j).start())
+        across(j).start()
+
+        @pl.loop(0, half // tile)
+        def _(t):
+            start = pl.multiple_of(t * tile, tile)
+            at = pl.ds(start, tile)
+            deeper = [
+                ein[j, part, at, :].astype(f32)
+                + jnp.where(core == 0, srecv[j, part, at, :].astype(f32), 0.0)
+                for part in range(2)
+            ]
+            put_tail(j, pl.multiple_of(core * half + start, tile), deeper)
+
+    def finish(j):
+        across(j).wait_recv()
+
+        @pl.loop(0, half // tile)
+        def _(t):
+            start = pl.multiple_of(t * tile, tile)
+            at = pl.ds(start, tile)
+            deeper = [xrecv[j, part, at, :].astype(f32) for part in range(2)]
+            put_tail(j, pl.multiple_of((1 - core) * half + start, tile), deeper)
+
+    block = 2 * width
+    blocks = size // block
+
+    def middle(h):
+        lanes = pl.ds(h * block, block)
+        for l in range(local):
+            @pl.loop(0, 2 * cols // 2)
+            def _(t):
+                at = pl.ds(pl.multiple_of(t * 2 * rows, 2 * rows), 2 * rows)
+                low = pl.ds(pl.multiple_of(2 * size * l + t * 2 * rows, 2 * rows), 2 * rows)
+                prod[low, lanes] = jnp.dot(
+                    ml[l, at, :], ts[l, :, lanes], preferred_element_type=f32
+                ).astype(bf16)
+
+    for j in range(chunks):
+        phase(j)
+        chain(j)
+        if j > 0:
+            finish(j - 1)
+    for h in range(blocks - 1):
+        middle(h)
+    finish(chunks - 1)
+    middle(blocks - 1)
+
+    tiles = 2 * rings
+    order = [(z // 2 + 1 + i) % blocks for i in range(blocks)]
+
+    def pair(i):
+        return remote(psend.at[i], precv.at[i], p_send.at[i], p_recv.at[i], other_core)
+
+    for i, h in enumerate(order):
+        lanes = pl.ds(pl.multiple_of(h * block, block), block)
+
+        @pl.loop(0, tiles)
+        def _(t):
+            at = pl.ds(pl.multiple_of(t * 2 * rows, 2 * rows), 2 * rows)
+            pacc[i, t] = jnp.dot(tl[at, :], prod[:, lanes], preferred_element_type=f32)
+            theirs = pl.ds(pl.multiple_of((1 - core) * rows, rows), rows)
+            psend[i, t] = pacc[i, t, theirs, :].astype(bf16)
+
+        pair(i).start()
+
+    def to_level(target):
+        return remote(
+            qsend.at[target], qrecv.at[z], q_send.at[target], q_recv.at[z],
+            device(target, x, y, core),
+        )
+
+    for i, h in enumerate(order):
+        pair(i).wait_recv()
+        for s in range(2):
+            target = h * 2 + s
+            lanes = pl.ds(s * width, width)
+
+            @pl.loop(0, tiles)
+            def _(t):
+                mine = pl.ds(pl.multiple_of(core * rows, rows), rows)
+                q = pacc[i, t, mine, lanes] + precv[i, t, :, lanes].astype(f32)
+                qsend[target, t] = q.astype(bf16)
+
+                @pl.when(target == z)
+                def _():
+                    qsum[t] = q
+
+            pl.when(target != z)(lambda: to_level(target).start())
+
+    for dz in range(1, levels):
+        source = (z + dz) % levels
+        remote(
+            qsend.at[source], qrecv.at[source], q_send.at[source], q_recv.at[source],
+            device(source, x, y, core),
+        ).wait_recv()
+
+        @pl.loop(0, tiles)
+        def _(t):
+            qsum[t] += qrecv[source, t].astype(f32)
+
+    @pl.loop(0, tiles)
+    def _(t):
+        fsend[t % rings, t // rings] = qsum[t].astype(bf16)
+
+    me = y * 2 + x
+
+    def to_rows(dx, dy):
+        xx, yy = (x + dx) % 2, (y + dy) % rings
+        return remote(
+            fsend.at[yy], frecv.at[me], f_send.at[dy * 2 + dx], f_recv.at[me],
+            device(z, xx, yy, core),
+        )
+
+    narrow = width // 2
+
+    def emit(w, part, value):
+        out[w, part] = jnp.where(x == 0, value[:, :narrow], value[:, narrow:])
+
+    for dx, dy in routes:
+        if dx or dy:
+            to_rows(dx, dy).start()
+    for part in range(2):
+        emit(me, part, qsum[part * rings + y])
+    for dx, dy in reversed(routes):
+        if dx or dy:
+            xx, yy = (x + dx) % 2, (y + dy) % rings
+            w = yy * 2 + xx
+            remote(
+                fsend.at[yy], frecv.at[w], f_send.at[dy * 2 + dx], f_recv.at[w],
+                device(z, xx, yy, core),
+            ).wait_recv()
+            for part in range(2):
+                emit(w, part, frecv[w, part].astype(f32))
+
+    for j in range(chunks):
+        for dx, dy in routes:
+            if dx or dy:
+                spread(j, dx, dy).wait_send()
+            else:
+                pl.when(core != x)(lambda: spread(j, dx, dy).wait_send())
+        share(j).wait_send()
+        pl.when(z > 0)(lambda: down(j).wait_send())
+        across(j).wait_send()
+    for i in range(blocks):
+        pair(i).wait_send()
+    for dz in range(1, levels):
+        to_level((z + dz) % levels).wait_send()
+    for dx, dy in routes:
+        if dx or dy:
+            to_rows(dx, dy).wait_send()
+
+
+def fused(recorded, vertical):
+    freqs, local, _, rows, size = recorded.shape
+    depths, cols = lax.axis_size("depth"), lax.axis_size("col")
+    levels, chunks_wide = depths // 2, 2 * size // depths
+    depth, col = lax.axis_index("depth"), lax.axis_index("col")
+    z, x, y, core = depth // 2, depth % 2, col // 2, col % 2
+    wave = lax.dynamic_index_in_dim(vertical, y * 2 + x, 0, keepdims=False)
+    index = ((z * 2 + core) * local + jnp.arange(local, dtype=jnp.int32)).astype(jnp.float32)
+    angle = wave[None] * index[:, None]
+    table = jnp.stack([jnp.cos(angle), jnp.sin(angle)], axis=1).reshape(2 * local, size)
+    width = chunks_wide
+    chunks, half, tiles, blocks = size // width, size // 2, cols, size // (2 * width)
+    sizes = (levels, freqs, cols, local, rows, size, width)
+    f32, bf16 = jnp.float32, jnp.bfloat16
+    dma = pltpu.SemaphoreType.DMA
+    return pl.pallas_call(
+        functools.partial(kernel, sizes),
+        out_shape=jax.ShapeDtypeStruct((freqs, 2, rows, size // depths), f32),
+        in_specs=[
+            pl.BlockSpec(memory_space=pl.ANY),
+            pl.BlockSpec(memory_space=pltpu.VMEM),
+            pl.BlockSpec(memory_space=pltpu.VMEM),
+        ],
+        out_specs=pl.BlockSpec(memory_space=pltpu.VMEM),
+        scratch_shapes=[
+            pltpu.VMEM((local, 2, size, size), bf16),
+            pltpu.VMEM((local, 2 * size, 2 * size), bf16),
+            pltpu.VMEM((2 * size, local * 2 * size), bf16),
+            pltpu.VMEM((local, 2 * size, size), bf16),
+            pltpu.VMEM((local * 2 * size, size), bf16),
+            pltpu.VMEM((local - 1, 2, size, size), f32),
+            pltpu.VMEM((chunks, 2, size, width), bf16),
+            pltpu.VMEM((chunks, 2, half, width), bf16),
+            pltpu.VMEM((chunks, 2, half, width), bf16),
+            pltpu.VMEM((chunks, 2, half, width), bf16),
+            pltpu.VMEM((chunks, 2, half, width), bf16),
+            pltpu.VMEM((chunks, 2, half, width), bf16),
+            pltpu.VMEM((blocks, tiles, 2 * rows, 2 * width), f32),
+            pltpu.VMEM((blocks, tiles, rows, 2 * width), bf16),
+            pltpu.VMEM((blocks, tiles, rows, 2 * width), bf16),
+            pltpu.VMEM((levels, tiles, rows, width), bf16),
+            pltpu.VMEM((levels, tiles, rows, width), bf16),
+            pltpu.VMEM((tiles, rows, width), f32),
+            pltpu.VMEM((cols // 2, 2, rows, width), bf16),
+            pltpu.VMEM((freqs, 2, rows, width), bf16),
+            dma((chunks, cols)), dma((chunks, cols)),
+            dma((chunks,)), dma((chunks,)),
+            dma((chunks,)), dma((chunks,)),
+            dma((chunks,)), dma((chunks,)),
+            dma((blocks,)), dma((blocks,)),
+            dma((levels,)), dma((levels,)),
+            dma((cols,)), dma((freqs,)),
+        ],
+        compiler_params=pltpu.CompilerParams(
+            collective_id=0, has_side_effects=True, vmem_limit_bytes=56 * 1024 * 1024
+        ),
+        name="prediction",
+    )(recorded, table.T, table * (1.0 / (depths * local)))
+
+
+def body(recorded, vertical):
+    freqs, local, _, rows, size = recorded.shape
+    depths, cols = lax.axis_size("depth"), lax.axis_size("col")
+    fits = cols == freqs and cols % 2 == 0 and depths % 4 == 0 and local > 1
+    fits = fits and rows % 128 == 0 and (2 * size // depths) % 128 == 0
+    return fused(recorded, vertical) if fits else shards(recorded, vertical)
+
+
 def solution(mesh):
     in_specs = (P(None, "depth", None, "col", None), P())
     out_specs = P(None, None, "col", "depth")
-    return jax.shard_map(shards, mesh=mesh, in_specs=in_specs, out_specs=out_specs, check_vma=False)
+    return jax.shard_map(body, mesh=mesh, in_specs=in_specs, out_specs=out_specs, check_vma=False)

time: 491 us -> 77.7 us (0.16)
  waiting for transfers between devices: 404 us -> 0 us
  Pallas kernels: 0 us -> 73.1 us
  other arithmetic: 41.5 us -> 0.82 us
  between operations: 14 us -> 0.02 us
  matrix products: 10.9 us -> 0 us
  local copies, waits for them, and re-layouts: 13.9 us -> 3.5 us
    all_gather x3 -> x0, waiting for transfers between devices: 282 us -> none  [the longest x1 223 us: prefix(): everything = lax.all_gather(x, axis)]
    unnamed x5 -> x0, waiting for transfers between devices: 100 us -> none
    pallas_call x0 -> x1, Pallas kernels: none -> 73.1 us  [fused(): pl.pallas_call(functools.partial(kernel, sizes), out_shape=jax.ShapeDtype...]
    ppermute x1 -> x0, waiting for transfers between devices: 22.2 us -> none  [from_behind(): lax.ppermute(value, axis, [(source, source + steps) for source in range(i...]
    select_n x8 -> x0, other arithmetic: 19.7 us -> none  [lap(): return jnp.where(reached, new, before)]
    dot_general x8 -> x0, matrix products: 10.9 us -> none  [the longest x2 4.15 us: complex_product(): jnp.einsum(pattern, left_imag, right_real, preferred_element_type=jnp.flo...]
    sub x1 -> x0, other arithmetic: 10.4 us -> none  [shards(): real_in * cosine - imag_in * sine_part]
  transfers between devices with their start and end apart: 5 -> 0, of which waited for: 5 -> 0; matrix products, arithmetic and copies ran while one was open for 8% -> 0% of each run, Pallas kernels for 0% -> 0%
where the time goes in v1:
time: 77.7 us; the launch traced here: 77.4 us
  Pallas kernels  73.1 us (94%)
  local copies, waits for them, and re-layouts  3.5 us (5%)
  other arithmetic  0.82 us (1%)
    pallas_call x1, Pallas kernels, fused(): pl.pallas_call(functools.partial(kernel, sizes), out_shape=jax.ShapeDtype...  73.1 us
    pallas_call x1, local copies, waits for them, and re-layouts, fused(): pl.pallas_call(functools.partial(kernel, sizes), out_shape=jax.ShapeDtype...  1.93 us

profile of v1, /device:TPU:8, one launch (start us, length us, event | category | flops | bytes accessed | tf_op | source)
XLA Modules:
  0.0 77.4 jit_solution(7547051673478655312)
XLA Ops:
  0.0 0.0 copy-start
  0.0 0.7 copy-done
  0.7 0.2 multiply_cosine_fusion
  0.9 0.6 broadcast_multiply_fusion.rt
  1.5 0.9 %copy.3.ct = f32[512,4]{1,0:T(8,128)} copy(f32[512,4]{0,1:T(4,128)S(1)} %bitcast.2) | data formatting | bytes 16384 | tf_op jit(solution)/shard_map/transpose | solution.py:452
  2.4 73.1 %prediction.1 = f32[4,2,128,64]{3,2,1,0:T(8,128)} custom-call(bf16[4,2,2,128,512]{4,3,2,1,0:T(8,128)(2,1)} %rec.1, f32[512,4]{1,0:T(8,128)} %copy.3.ct, f32[4,512]{1,0:T(4,128)} %broadcast_multiply_fusion.rt), custom_call_target="tpu_custom_call" | custom-call | tf_op jit(solution)/shard_map/prediction/pallas_call | solution.py:410
  75.5 1.9 %copy.4 = f32[4,2,128,64]{2,3,1,0:T(8,128)} copy(f32[4,2,128,64]{3,2,1,0:T(8,128)} %prediction.1) | data formatting | bytes 524288 | tf_op jit(solution)/shard_map/prediction/pallas_call | solution.py:410
  (4 shorter events, 0.0 us)
Async XLA Ops:
  0.0 0.7 copy-start

commit v2 on v1

--- a/solution.py
+++ b/solution.py
@@ -8,6 +8,7 @@
 from jax.sharding import PartitionSpec as P
 
 MESH = pl.DeviceIdType.MESH
+SPLITS = 2
 
 
 def prefix(x, axis, combine, identity):
@@ -94,24 +95,28 @@
 
 
 def kernel(
-    sizes, rec, ct, rt, out, land, ml, tl, ts, prod, suf, sbuf, srecv, ein, eout, xsend, xrecv,
+    sizes, rec, vertical, out, waves, table, ct, rt, land, ml, tl, ts, prod, suf, sbuf, srecv, ein, eout, xsend, xrecv,
     pacc, psend, precv, qsend, qrecv, qsum, fsend, frecv,
-    a_send, a_recv, s_send, s_recv, e_send, e_recv, x_send, x_recv, p_send, p_recv,
+    v_sem, a_send, a_recv, s_send, s_recv, e_send, e_recv, x_send, x_recv, p_send, p_recv,
     q_send, q_recv, f_send, f_recv,
 ):
-    levels, freqs, cols, local, rows, size, width = sizes
+    levels, freqs, cols, local, rows, size, width, splits = sizes
     depth, col = lax.axis_index("depth"), lax.axis_index("col")
     z, x = depth // 2, depth % 2
     y, core = col // 2, col % 2
     rings = cols // 2
-    half = size // 2
     chunks = size // width
+    sub = rows // splits
+    share_rows = cols * sub // 2
+    me = y * 2 + x
     f32, bf16 = jnp.float32, jnp.bfloat16
 
     def device(zz, xx, yy, cc):
         return (zz * 2 + xx, yy * 2 + cc)
 
     other_core = device(z, x, y, 1 - core)
+    fetch = pltpu.make_async_copy(vertical, waves, v_sem)
+    fetch.start()
     barrier = pltpu.get_barrier_semaphore()
     greeted = 0
     for dx in range(2):
@@ -134,39 +139,54 @@
             src_ref=src, dst_ref=dst, send_sem=send, recv_sem=recv, device_id=to, device_id_type=MESH
         )
 
-    def spread(j, dx, dy, near=False):
+    pieces = [(j, r) for j in range(chunks) for r in range(splits)]
+
+    def spread(n, dx, dy, near=False):
+        j, r = pieces[n]
         xx, yy = (x + dx) % 2, (y + dy) % rings
         w = yy * 2 + xx
-        src = rec.at[w, :, :, :, pl.ds(j * width, width)]
-        dst = land.at[:, :, pl.ds(pl.multiple_of(col * rows, rows), rows), pl.ds(j * width, width)]
+        lanes = pl.ds(j * width, width)
+        src = rec.at[w, :, :, pl.ds(r * sub, sub), lanes]
+        dst = land.at[:, :, pl.ds(pl.multiple_of(col * rows + r * sub, sub), sub), lanes]
         if near:
-            return pltpu.make_async_copy(src, dst, a_recv.at[j, col])
-        return remote(src, dst, a_send.at[j, dy * 2 + dx], a_recv.at[j, col], device(z, xx, yy, x))
+            return pltpu.make_async_copy(src, dst, a_recv.at[n, col])
+        return remote(src, dst, a_send.at[n, dy * 2 + dx], a_recv.at[n, col], device(z, xx, yy, x))
 
     routes = [(dx, dy) for dy in reversed(range(rings)) for dx in (1, 0)]
-    for j in range(chunks):
+    for n in range(len(pieces)):
         for dx, dy in routes:
             if dx or dy:
-                spread(j, dx, dy).start()
+                spread(n, dx, dy).start()
             else:
-                pl.when(core == x)(lambda: spread(j, dx, dy, near=True).start())
-                pl.when(core != x)(lambda: spread(j, dx, dy).start())
+                pl.when(core == x)(lambda: spread(n, dx, dy, near=True).start())
+                pl.when(core != x)(lambda: spread(n, dx, dy).start())
 
     @pl.when(z == levels - 1)
     def _():
         ein[...] = jnp.zeros_like(ein)
 
-    tile = 64
-
-    def phase(j):
+    fetch.wait()
+    wave = waves[pl.ds(me, 1), :]
+    table[...] = jnp.zeros_like(table)
+    for l in range(local):
+        angle = wave * ((z * 2 + core) * local + l).astype(f32)
+        table[2 * l : 2 * l + 1, :] = jnp.cos(angle)
+        table[2 * l + 1 : 2 * l + 2, :] = jnp.sin(angle)
+    ct[...] = table[...].T
+    rt[...] = table[0 : 2 * local, :] * (1.0 / (2 * levels * local))
+
+    tile = sub
+
+    def phase(n):
+        j, r = pieces[n]
         for source in range(cols):
-            dst = land.at[:, :, pl.ds(source * rows, rows), pl.ds(j * width, width)]
-            pltpu.make_async_copy(dst, dst, a_recv.at[j, source]).wait()
+            dst = land.at[:, :, pl.ds(source * rows + r * sub, sub), pl.ds(j * width, width)]
+            pltpu.make_async_copy(dst, dst, a_recv.at[n, source]).wait()
         lanes = pl.ds(j * width, width)
 
-        @pl.loop(0, size // tile)
-        def _(t):
-            start = pl.multiple_of(t * tile, tile)
+        @pl.loop(0, cols)
+        def _(t):
+            start = pl.multiple_of(t * rows + r * sub, sub)
             at = pl.ds(start, tile)
             low = pl.ds(start + size, tile)
             sum_re = sum_im = None
@@ -190,13 +210,14 @@
                 plus_re, plus_im = a - b, c + d
                 sum_re = plus_re if sum_re is None else sum_re + plus_re
                 sum_im = plus_im if sum_im is None else sum_im + plus_im
-            sbuf[j, 0, at, :] = sum_re.astype(bf16)
-            sbuf[j, 1, at, :] = sum_im.astype(bf16)
-
-        share(j).start()
+            packed = pl.ds(pl.multiple_of(t * sub, sub), sub)
+            sbuf[n, 0, packed, :] = sum_re.astype(bf16)
+            sbuf[n, 1, packed, :] = sum_im.astype(bf16)
+
+        share(n).start()
 
     def share(j):
-        theirs = pl.ds(pl.multiple_of((1 - core) * half, half), half)
+        theirs = pl.ds(pl.multiple_of((1 - core) * share_rows, share_rows), share_rows)
         return remote(sbuf.at[j, :, theirs, :], srecv.at[j], s_send.at[j], s_recv.at[j], other_core)
 
     def down(j):
@@ -206,7 +227,8 @@
     def across(j):
         return remote(xsend.at[j], xrecv.at[j], x_send.at[j], x_recv.at[j], other_core)
 
-    def put_tail(j, start, deeper):
+    def put_tail(n, start, deeper):
+        j = pieces[n][0]
         at, low = pl.ds(start, tile), pl.ds(start + size, tile)
         lanes = pl.ds(j * width, width)
         for l in range(local):
@@ -223,45 +245,47 @@
             tl[at, second] = (-im).astype(bf16)
             tl[low, first] = im.astype(bf16)
 
-    def chain(j):
-        share(j).wait_recv()
-        pl.when(z < levels - 1)(lambda: down(j).wait_recv())
-
-        @pl.loop(0, half // tile)
-        def _(t):
-            start = pl.multiple_of(t * tile, tile)
-            at = pl.ds(start, tile)
-            mine = pl.ds(pl.multiple_of(core * half + start, tile), tile)
+    def chain(n):
+        r = pieces[n][1]
+        share(n).wait_recv()
+        pl.when(z < levels - 1)(lambda: down(n).wait_recv())
+
+        @pl.loop(0, cols // 2)
+        def _(t):
+            start = pl.multiple_of(t * sub, sub)
+            at = pl.ds(start, sub)
+            mine = pl.ds(pl.multiple_of(core * share_rows + start, sub), sub)
             for part in range(2):
-                below = ein[j, part, at, :].astype(f32)
-                own = sbuf[j, part, mine, :].astype(f32)
-                their = srecv[j, part, at, :].astype(f32)
-                eout[j, part, at, :] = (below + own + their).astype(bf16)
-                xsend[j, part, at, :] = (below + jnp.where(core == 1, own, 0.0)).astype(bf16)
-
-        pl.when(z > 0)(lambda: down(j).start())
-        across(j).start()
-
-        @pl.loop(0, half // tile)
-        def _(t):
-            start = pl.multiple_of(t * tile, tile)
-            at = pl.ds(start, tile)
+                below = ein[n, part, at, :].astype(f32)
+                own = sbuf[n, part, mine, :].astype(f32)
+                their = srecv[n, part, at, :].astype(f32)
+                eout[n, part, at, :] = (below + own + their).astype(bf16)
+                xsend[n, part, at, :] = (below + jnp.where(core == 1, own, 0.0)).astype(bf16)
+
+        pl.when(z > 0)(lambda: down(n).start())
+        across(n).start()
+
+        @pl.loop(0, cols // 2)
+        def _(t):
+            at = pl.ds(pl.multiple_of(t * sub, sub), sub)
             deeper = [
-                ein[j, part, at, :].astype(f32)
-                + jnp.where(core == 0, srecv[j, part, at, :].astype(f32), 0.0)
+                ein[n, part, at, :].astype(f32)
+                + jnp.where(core == 0, srecv[n, part, at, :].astype(f32), 0.0)
                 for part in range(2)
             ]
-            put_tail(j, pl.multiple_of(core * half + start, tile), deeper)
-
-    def finish(j):
-        across(j).wait_recv()
-
-        @pl.loop(0, half // tile)
-        def _(t):
-            start = pl.multiple_of(t * tile, tile)
-            at = pl.ds(start, tile)
-            deeper = [xrecv[j, part, at, :].astype(f32) for part in range(2)]
-            put_tail(j, pl.multiple_of((1 - core) * half + start, tile), deeper)
+            start = (core * (cols // 2) + t) * rows + r * sub
+            put_tail(n, pl.multiple_of(start, sub), deeper)
+
+    def finish(n):
+        r = pieces[n][1]
+        across(n).wait_recv()
+
+        @pl.loop(0, cols // 2)
+        def _(t):
+            at = pl.ds(pl.multiple_of(t * sub, sub), sub)
+            deeper = [xrecv[n, part, at, :].astype(f32) for part in range(2)]
+            start = ((1 - core) * (cols // 2) + t) * rows + r * sub
+            put_tail(n, pl.multiple_of(start, sub), deeper)
 
     block = 2 * width
     blocks = size // block
@@ -277,14 +301,23 @@
                     ml[l, at, :], ts[l, :, lanes], preferred_element_type=f32
                 ).astype(bf16)
 
-    for j in range(chunks):
-        phase(j)
-        chain(j)
-        if j > 0:
-            finish(j - 1)
-    for h in range(blocks - 1):
-        middle(h)
-    finish(chunks - 1)
+    last = len(pieces) - 1
+
+    def early():
+        for h in range(blocks - 1):
+            middle(h)
+
+    for n in range(last):
+        phase(n)
+        chain(n)
+        if n > 0:
+            finish(n - 1)
+    phase(last)
+    finish(last - 1)
+    pl.when(z < levels - 1)(early)
+    chain(last)
+    pl.when(z == levels - 1)(early)
+    finish(last)
     middle(blocks - 1)
 
     tiles = 2 * rings
@@ -340,49 +373,46 @@
         def _(t):
             qsum[t] += qrecv[source, t].astype(f32)
 
-    @pl.loop(0, tiles)
-    def _(t):
-        fsend[t % rings, t // rings] = qsum[t].astype(bf16)
-
-    me = y * 2 + x
+    narrow = width // 2
+
+    def joined(yy, xx):
+        lanes = slice(xx * narrow, (xx + 1) * narrow)
+        return jnp.concatenate([qsum[yy][:, lanes], qsum[rings + yy][:, lanes]], axis=1)
+
+    for yy in range(rings):
+        for xx in range(2):
+            fsend[yy, xx] = joined(yy, xx).astype(bf16)
 
     def to_rows(dx, dy):
         xx, yy = (x + dx) % 2, (y + dy) % rings
         return remote(
-            fsend.at[yy], frecv.at[me], f_send.at[dy * 2 + dx], f_recv.at[me],
+            fsend.at[yy, xx], frecv.at[me], f_send.at[dy * 2 + dx], f_recv.at[me],
             device(z, xx, yy, core),
         )
-
-    narrow = width // 2
-
-    def emit(w, part, value):
-        out[w, part] = jnp.where(x == 0, value[:, :narrow], value[:, narrow:])
 
     for dx, dy in routes:
         if dx or dy:
             to_rows(dx, dy).start()
-    for part in range(2):
-        emit(me, part, qsum[part * rings + y])
+    out[me] = jnp.where(x == 0, joined(y, 0), joined(y, 1))
     for dx, dy in reversed(routes):
         if dx or dy:
             xx, yy = (x + dx) % 2, (y + dy) % rings
             w = yy * 2 + xx
             remote(
-                fsend.at[yy], frecv.at[w], f_send.at[dy * 2 + dx], f_recv.at[w],
+                fsend.at[yy, xx], frecv.at[w], f_send.at[dy * 2 + dx], f_recv.at[w],
                 device(z, xx, yy, core),
             ).wait_recv()
-            for part in range(2):
-                emit(w, part, frecv[w, part].astype(f32))
-
-    for j in range(chunks):
+            out[w] = frecv[w].astype(f32)
+
+    for n in range(len(pieces)):
         for dx, dy in routes:
             if dx or dy:
-                spread(j, dx, dy).wait_send()
+                spread(n, dx, dy).wait_send()
             else:
-                pl.when(core != x)(lambda: spread(j, dx, dy).wait_send())
-        share(j).wait_send()
-        pl.when(z > 0)(lambda: down(j).wait_send())
-        across(j).wait_send()
+                pl.when(core != x)(lambda: spread(n, dx, dy).wait_send())
+        share(n).wait_send()
+        pl.when(z > 0)(lambda: down(n).wait_send())
+        across(n).wait_send()
     for i in range(blocks):
         pair(i).wait_send()
     for dz in range(1, levels):
@@ -396,39 +426,37 @@
     freqs, local, _, rows, size = recorded.shape
     depths, cols = lax.axis_size("depth"), lax.axis_size("col")
     levels, chunks_wide = depths // 2, 2 * size // depths
-    depth, col = lax.axis_index("depth"), lax.axis_index("col")
-    z, x, y, core = depth // 2, depth % 2, col // 2, col % 2
-    wave = lax.dynamic_index_in_dim(vertical, y * 2 + x, 0, keepdims=False)
-    index = ((z * 2 + core) * local + jnp.arange(local, dtype=jnp.int32)).astype(jnp.float32)
-    angle = wave[None] * index[:, None]
-    table = jnp.stack([jnp.cos(angle), jnp.sin(angle)], axis=1).reshape(2 * local, size)
     width = chunks_wide
-    chunks, half, tiles, blocks = size // width, size // 2, cols, size // (2 * width)
-    sizes = (levels, freqs, cols, local, rows, size, width)
+    chunks, tiles, blocks = size // width, cols, size // (2 * width)
+    pieces, share_rows = chunks * SPLITS, rows * cols // SPLITS // 2
+    sizes = (levels, freqs, cols, local, rows, size, width, SPLITS)
     f32, bf16 = jnp.float32, jnp.bfloat16
     dma = pltpu.SemaphoreType.DMA
-    return pl.pallas_call(
+    packed = pl.pallas_call(
         functools.partial(kernel, sizes),
-        out_shape=jax.ShapeDtypeStruct((freqs, 2, rows, size // depths), f32),
+        out_shape=jax.ShapeDtypeStruct((freqs, rows, width), f32),
         in_specs=[
             pl.BlockSpec(memory_space=pl.ANY),
-            pl.BlockSpec(memory_space=pltpu.VMEM),
-            pl.BlockSpec(memory_space=pltpu.VMEM),
+            pl.BlockSpec(memory_space=pl.ANY),
         ],
         out_specs=pl.BlockSpec(memory_space=pltpu.VMEM),
         scratch_shapes=[
+            pltpu.VMEM((freqs, size), f32),
+            pltpu.VMEM((128, size), f32),
+            pltpu.VMEM((size, 128), f32),
+            pltpu.VMEM((2 * local, size), f32),
             pltpu.VMEM((local, 2, size, size), bf16),
             pltpu.VMEM((local, 2 * size, 2 * size), bf16),
             pltpu.VMEM((2 * size, local * 2 * size), bf16),
             pltpu.VMEM((local, 2 * size, size), bf16),
             pltpu.VMEM((local * 2 * size, size), bf16),
             pltpu.VMEM((local - 1, 2, size, size), f32),
-            pltpu.VMEM((chunks, 2, size, width), bf16),
-            pltpu.VMEM((chunks, 2, half, width), bf16),
-            pltpu.VMEM((chunks, 2, half, width), bf16),
-            pltpu.VMEM((chunks, 2, half, width), bf16),
-            pltpu.VMEM((chunks, 2, half, width), bf16),
-            pltpu.VMEM((chunks, 2, half, width), bf16),
+            pltpu.VMEM((pieces, 2, 2 * share_rows, width), bf16),
+            pltpu.VMEM((pieces, 2, share_rows, width), bf16),
+            pltpu.VMEM((pieces, 2, share_rows, width), bf16),
+            pltpu.VMEM((pieces, 2, share_rows, width), bf16),
+            pltpu.VMEM((pieces, 2, share_rows, width), bf16),
+            pltpu.VMEM((pieces, 2, share_rows, width), bf16),
             pltpu.VMEM((blocks, tiles, 2 * rows, 2 * width), f32),
             pltpu.VMEM((blocks, tiles, rows, 2 * width), bf16),
             pltpu.VMEM((blocks, tiles, rows, 2 * width), bf16),
@@ -436,11 +464,11 @@
             pltpu.VMEM((levels, tiles, rows, width), bf16),
             pltpu.VMEM((tiles, rows, width), f32),
             pltpu.VMEM((cols // 2, 2, rows, width), bf16),
-            pltpu.VMEM((freqs, 2, rows, width), bf16),
-            dma((chunks, cols)), dma((chunks, cols)),
-            dma((chunks,)), dma((chunks,)),
-            dma((chunks,)), dma((chunks,)),
-            dma((chunks,)), dma((chunks,)),
+            pltpu.VMEM((freqs, rows, width), bf16),
+            dma, dma((pieces, cols)), dma((pieces, cols)),
+            dma((pieces,)), dma((pieces,)),
+            dma((pieces,)), dma((pieces,)),
+            dma((pieces,)), dma((pieces,)),
             dma((blocks,)), dma((blocks,)),
             dma((levels,)), dma((levels,)),
             dma((cols,)), dma((freqs,)),
@@ -449,7 +477,8 @@
             collective_id=0, has_side_effects=True, vmem_limit_bytes=56 * 1024 * 1024
         ),
         name="prediction",
-    )(recorded, table.T, table * (1.0 / (depths * local)))
+    )(recorded, vertical)
+    return jnp.stack([packed[:, :, : width // 2], packed[:, :, width // 2 :]], axis=1)
 
 
 def body(recorded, vertical):

time: 77.7 us -> 69.3 us (0.89); the launches traced: 77.4 us -> 68 us
  Pallas kernels: 73.1 us -> 65.9 us
  local copies, waits for them, and re-layouts: 3.5 us -> 2.05 us
  other arithmetic: 0.82 us -> 0.04 us
    pallas_call x1, Pallas kernels: 73.1 us -> 65.9 us  [fused(): pl.pallas_call(functools.partial(kernel, sizes), out_shape=jax.ShapeDtype...]
    another operation x0 -> x2, local copies, waits for them, and re-layouts: none -> 2.05 us  [fused(): jnp.stack([packed[:, :, :width // 2], packed[:, :, width // 2:]], axis=1)]
    pallas_call x1 -> x0, local copies, waits for them, and re-layouts: 1.93 us -> none  [fused(): pl.pallas_call(functools.partial(kernel, sizes), out_shape=jax.ShapeDtype...]
    transpose x1 -> x0, local copies, waits for them, and re-layouts: 0.86 us -> none  [fused(): return pl.pallas_call(functools.partial(kernel, sizes), out_shape=jax.Sha...]
where the time goes in v2:
time: 69.3 us; the launch traced here: 68 us
  Pallas kernels  65.9 us (95%)
  local copies, waits for them, and re-layouts  2.05 us (3%)
    pallas_call x1, Pallas kernels, fused(): pl.pallas_call(functools.partial(kernel, sizes), out_shape=jax.ShapeDtype...  65.9 us
    another operation x2, local copies, waits for them, and re-layouts, fused(): jnp.stack([packed[:, :, :width // 2], packed[:, :, width // 2:]], axis=1)  2.05 us

profile of v2, /device:TPU:8, one launch (start us, length us, event | category | flops | bytes accessed | tf_op | source)
XLA Modules:
  0.0 68.0 jit_solution(17104018513995404280)
XLA Ops:
  0.0 65.9 %prediction.1 = f32[4,128,128]{2,1,0:T(8,128)} custom-call(bf16[4,2,2,128,512]{4,3,2,1,0:T(8,128)(2,1)} %rec.1, f32[4,512]{1,0:T(4,128)} %vertical.1), custom_call_target="tpu_custom_call" | custom-call | tf_op jit(solution)/shard_map/prediction/pallas_call | solution.py:435
  65.9 1.2 %slice_bitcast_fusion.1 = (f32[4,1,128,64]{3,2,0,1:T(8,128)S(1)}, f32[4,1,128,64]{3,2,0,1:T(8,128)S(1)}) fusion(f32[4,128,128]{2,1,0:T(8,128)} %prediction.1), kind=kLoop, calls=%fused_computation.2 | loop fusion | bytes 524288 | tf_op jit(solution)/shard_map/stack | solution.py:481
  67.1 0.9 %copy.3 = f32[4,2,128,64]{2,3,1,0:T(8,128)} copy(f32[4,2,128,64]{3,2,0,1:T(8,128)S(1)} %pad_maximum_fusion) | data formatting | bytes 524288 | tf_op jit(solution)/shard_map/stack | solution.py:481
  (1 shorter events, 0.0 us)

commit v3 on v2

--- a/solution.py
+++ b/solution.py
@@ -8,7 +8,7 @@
 from jax.sharding import PartitionSpec as P
 
 MESH = pl.DeviceIdType.MESH
-SPLITS = 2
+SPLITS = 4
 
 
 def prefix(x, axis, combine, identity):
@@ -478,7 +478,7 @@
         ),
         name="prediction",
     )(recorded, vertical)
-    return jnp.stack([packed[:, :, : width // 2], packed[:, :, width // 2 :]], axis=1)
+    return packed.reshape(freqs, rows, 2, width // 2).transpose(0, 2, 1, 3)
 
 
 def body(recorded, vertical):

time: 69.3 us -> 68.3 us (0.986); the launches traced: 68 us -> 68.1 us
    another operation x2 -> x0, local copies, waits for them, and re-layouts: 2.05 us -> none  [fused(): jnp.stack([packed[:, :, :width // 2], packed[:, :, width // 2:]], axis=1)]
    pallas_call x0 -> x1, local copies, waits for them, and re-layouts: none -> 1.79 us  [fused(): pl.pallas_call(functools.partial(kernel, sizes), out_shape=jax.ShapeDtype...]
where the time goes in v3:
time: 68.3 us; the launch traced here: 68.1 us
  Pallas kernels  66.3 us (97%)
  local copies, waits for them, and re-layouts  1.79 us (3%)
    pallas_call x1, Pallas kernels, fused(): pl.pallas_call(functools.partial(kernel, sizes), out_shape=jax.ShapeDtype...  66.3 us
    pallas_call x1, local copies, waits for them, and re-layouts, fused(): pl.pallas_call(functools.partial(kernel, sizes), out_shape=jax.ShapeDtype...  1.79 us

profile of v3, /device:TPU:8, one launch (start us, length us, event | category | flops | bytes accessed | tf_op | source)
XLA Modules:
  0.0 68.1 jit_solution(12812215138300802949)
XLA Ops:
  0.0 66.3 %prediction.1 = f32[4,128,128]{2,1,0:T(8,128)} custom-call(bf16[4,2,2,128,512]{4,3,2,1,0:T(8,128)(2,1)} %rec.1, f32[4,512]{1,0:T(4,128)} %vertical.1), custom_call_target="tpu_custom_call" | custom-call | tf_op jit(solution)/shard_map/prediction/pallas_call | solution.py:435
  66.3 1.8 %copy.4 = f32[4,128,128]{1,2,0:T(8,128)} copy(f32[4,128,128]{2,1,0:T(8,128)} %prediction.1) | data formatting | bytes 524288 | tf_op jit(solution)/shard_map/prediction/pallas_call | solution.py:435
